TPU v7x, 256 devices: a whole 4x4x8 slice. The times are simulated.
256 devices in a mesh: shadow: 32 (over z, y_lo, core), vocab: 8 (over y_hi, x).
Axes of the slice: x: 4, y: 4 (y_hi: 2, y_lo: 2; y = y_hi * 2 + y_lo), z: 8, core: 2. Of those that a mesh axis runs over, the one named last changes fastest.
Arguments:
- hidden: bfloat16 [128, 128, 2048], P('shadow'), may hold values from -18 to 18
- targets: int32 [128], replicated, may hold values from 0 to 32767
- membership: int32 [128, 4], P('shadow'), may hold values from 0 to 1, as said below
- unembedding: bfloat16 [32768, 2048], P(('shadow', 'vocab')), may hold values from -1 to 1
Outputs:
- score: float32 [128, 128], P('shadow', 'vocab')
Inputs may be any that keep to these rules, and one draw needn't show every extreme that they name: `membership`: each candidate sequence is a member of exactly 64 of the shadow models.
All inputs are finite; a program needn't handle non-finite values.
Results may differ from a plain program's by a relative error of at most 0.00055.
Values may be sent and summed in bfloat16 or wider, within the bound.
No kernel may reach another device: no remote copies, remote signals or barrier semaphores. Data moves between devices by JAX's collectives and lax.ppermute only.
A program may use at most 64 MiB of HBM per device.

v0:
```python
import jax
import jax.numpy as jnp
from jax import lax
from jax.sharding import PartitionSpec as P

SEQ = 32
NEG_FILL = -1e30
VAR_FLOOR = 0.5


def copy_for_each(value, axis):
    copies = jnp.broadcast_to(value, (lax.axis_size(axis), *value.shape))
    return lax.all_to_all(copies, axis, split_axis=0, concat_axis=0, tiled=True)


def all_in_one(value, axis):
    leaves = jax.tree.leaves(value)
    sequence = sorted(range(len(leaves)), key=lambda k: -leaves[k].size)
    width = (1, *leaves[sequence[0]].shape)[-1]
    lines = [
        jnp.pad(leaves[k].reshape(-1), (0, -leaves[k].size % width)).reshape(-1, width)
        for k in sequence
    ]
    both, at, found = (copy_for_each(jnp.concatenate(lines), axis), 0, {})
    for k, line in zip(sequence, lines):
        share = both[:, at : at + len(line)].reshape(len(both), -1)
        found[k] = share[:, : leaves[k].size].reshape(-1, *leaves[k].shape)
        at += len(line)
    numbers = iter(range(len(leaves)))
    return jax.tree.map(lambda _: found[next(numbers)], value)


def folded_in_pairs(pieces, combine):
    while len(jax.tree.leaves(pieces)[0]) > 1:
        pieces = jax.vmap(combine)(
            *(jax.tree.map(lambda part: part[side::2], pieces) for side in (0, 1))
        )
    return jax.tree.map(lambda part: part[0], pieces)


def joined_all(value, axis, combine):
    pieces = all_in_one(value, axis)
    return folded_in_pairs(pieces, combine)


def over_copies(value, axis):
    everything = copy_for_each(value, axis)
    return jnp.sum(everything, axis=0)


def packed_total(arrays, axis):
    ends = [0]
    for a in arrays:
        ends.append(ends[-1] + a.size)
    total = over_copies(jnp.concatenate([a.ravel() for a in arrays]), axis)
    return tuple((total[b:e].reshape(a.shape) for a, b, e in zip(arrays, ends, ends[1:])))


def start_state(row_count):
    return (
        jnp.full((row_count,), NEG_FILL, jnp.float32),
        jnp.zeros((row_count,), jnp.float32),
        jnp.zeros((row_count,), jnp.float32),
    )


def fold_block(running, flat_rows, wanted, block_rows, vocab_rows):
    highest, summed, target_logit = running
    logits = lax.dot_general(
        flat_rows, block_rows, (((1,), (1,)), ((), ())), preferred_element_type=jnp.float32
    )
    target_hit = wanted[:, None] == vocab_rows[None, :]
    target_logit = jnp.sum(jnp.where(target_hit, logits, 0.0), axis=1)
    others = jnp.where(target_hit, NEG_FILL, logits)
    raised = jnp.maximum(highest, jnp.max(others, axis=1))
    fresh_terms = jnp.where(target_hit, 0.0, jnp.exp(others - raised[:, None]))
    summed = jnp.sum(fresh_terms, axis=1)
    return (raised, summed, target_logit)


def combine_pairs(earlier, latter):
    raised = jnp.maximum(earlier[0], latter[0])
    summed = earlier[1] * jnp.exp(earlier[0] - raised) + latter[1] * jnp.exp(latter[0] - raised)
    return (raised, summed, earlier[2] + latter[2])


def per_device(hidden, targets, membership, unembedding):
    shadow_count, token_count, model_width = hidden.shape
    head_rows = unembedding.shape[0]
    vocab_count = lax.axis_size("vocab")
    vocab_index = lax.axis_index("vocab")
    shadows_total = shadow_count * lax.axis_size("shadow")
    slice_tokens = token_count // vocab_count
    slice_start = vocab_index * slice_tokens
    flat_rows = hidden.reshape(shadow_count * token_count, model_width)
    wanted = jnp.tile(targets, shadow_count)
    block_rows = lax.all_gather(unembedding, "shadow", axis=0, tiled=True)
    gathered = jnp.arange(block_rows.shape[0], dtype=jnp.int32)
    vocab_rows = (
        gathered // head_rows * vocab_count + vocab_index
    ) * head_rows + gathered % head_rows
    highest, summed, target_logit = fold_block(
        start_state(flat_rows.shape[0]), flat_rows, wanted, block_rows, vocab_rows
    )
    highest, summed, target_logit = joined_all(
        (highest, summed, target_logit), "vocab", combine_pairs
    )
    all_confidence = (target_logit - (highest + jnp.log(summed))).reshape(shadow_count, token_count)
    confidence = lax.dynamic_slice_in_dim(all_confidence, slice_start, slice_tokens, 1)
    member_tokens = jnp.repeat(membership, SEQ, axis=1)
    outside = (1 - lax.dynamic_slice_in_dim(member_tokens, slice_start, slice_tokens, 1)).astype(
        jnp.float32
    )
    weighted = outside * confidence
    first_moment, second_moment = packed_total(
        (jnp.sum(weighted, axis=0), jnp.sum(weighted * confidence, axis=0)), "shadow"
    )
    out_count = shadows_total // 2 - outside
    out_mean = (first_moment[None, :] - weighted) / out_count
    out_variance = (
        second_moment[None, :] - weighted * confidence
    ) / out_count - out_mean * out_mean
    return (confidence - out_mean) * lax.rsqrt(jnp.maximum(out_variance, 0.0) + VAR_FLOOR)


def solution(mesh):
    return jax.shard_map(
        per_device,
        mesh=mesh,
        in_specs=(P("shadow", None, None), P(), P("shadow", None), P(("shadow", "vocab"), None)),
        out_specs=P("shadow", "vocab"),
        check_vma=False,
    )
```

profile of v0, /device:TPU:1, one launch (start us, length us, event | category | flops | bytes accessed | tf_op | source)
XLA Modules:
  0.0 166.2 jit_solution(9505137555500328018)
XLA Ops:
  6.5 0.0 copy-start
  6.5 0.0 all-gather.2.cloned.1.call-start
  6.5 0.7 all-gather.2.cloned.1.call-update
  7.3 0.7 broadcast_bitcast_fusion
  7.9 105.2 %all-gather.2.cloned.1.call-done = bf16[4096,2048]{1,0:T(8,128)(2,1)} async-done(((bf16[128,2048]{1,0:T(8,128)(2,1)}), bf16[4096,2048]{1,0:T(8,128)(2,1)}) %all-gather.2.cloned.1.call-update) | async-done | bytes 16777232 | tf_op jit(solution)/shard_map/all_gather | solution.py:97
  113.1 0.0 copy-done
  113.1 12.0 %fusion.2 = (f32[512]{0:T(512)S(1)}, f32[512,4096]{1,0:T(8,128)S(1)}) fusion(s32[4096]{0:T(1024)S(1)} %fusion.12, s32[512]{0:T(512)S(1)} %broadcast_bitcast_fusion, bf16[512,2048]{1,0:T(8,128)(2,1)S(1)} %bitcast.17, bf16[4096,2048]{1,0:T(8,128)(2,1)} %all-gather.2.cloned.1.call-done), kind=kOutput, calls=%fused_computation.5 | convolution fusion | flops 8596226048 | bytes 27283456 | tf_op jit(solution)/shard_map/dot_general | solution.py:69
  125.1 0.0 copy-start.1
  125.2 3.4 %fusion = (f32[512]{0:T(512)S(1)}, f32[512]{0:T(512)S(1)}) fusion(f32[512,4096]{1,0:T(8,128)S(1)} %get-tuple-element.19, f32[512]{0:T(512)S(1)} %broadcast_maximum_fusion, s32[4096]{0:T(1024)S(1)} %fusion.12, s32[512]{0:T(512)S(1)} %broadcast_bitcast_fusion), kind=kLoop, calls=%fused_computation.3 | loop fusion | flops 14679040 | bytes 8413184 | tf_op jit(solution)/shard_map/reduce_sum | solution.py:77
  128.6 0.6 broadcast_in_dim.28
  129.2 6.4 %all-to-all-start = ((f32[8,3,512]{2,1,0:T(4,128)}), f32[8,3,512]{2,1,0:T(4,128)S(1)}, u32[]{:S(2)}, u32[]{:S(2)}) async-start(f32[8,3,512]{2,1,0:T(4,128)} %broadcast_in_dim.28), calls=%async_computation | async-start | bytes 131072 | tf_op jit(solution)/shard_map/all_to_all | solution.py:13
  135.6 0.0 copy-done.1
  135.7 0.1 broadcast_in_dim.29
  135.7 0.1 reshape.79
  135.8 6.5 %all-to-all-done = f32[8,3,512]{2,1,0:T(4,128)S(1)} async-done(((f32[8,3,512]{2,1,0:T(4,128)}), f32[8,3,512]{2,1,0:T(4,128)S(1)}, u32[]{:S(2)}, u32[]{:S(2)}) %all-to-all-start) | async-done | bytes 49184 | tf_op jit(solution)/shard_map/all_to_all | solution.py:13
  142.8 0.1 fusion.17
  142.9 0.1 pad_maximum_fusion.1
  143.0 15.7 %all_to_all.11 = f32[32,1,32]{2,1,0:T(1,128)S(1)} all-to-all(f32[32,1,32]{2,1,0:T(1,128)S(1)} %broadcast_in_dim.30), channel_id=1, replica_groups=mesh['shadow'=32,'vocab'=8] {'shadow'}, dimensions={0} | all-to-all | bytes 8192 | tf_op jit(solution)/shard_map/all_to_all | solution.py:13
  158.6 0.1 fusion.21
  158.7 0.7 rsqrt_multiply_fusion
  (25 shorter events, 0.5 us)
Async XLA Ops:
  6.5 106.6 %copy-start = (bf16[4,128,2048]{2,1,0:T(8,128)(2,1)S(1)}, bf16[4,128,2048]{2,1,0:T(8,128)(2,1)}, u32[]{:S(2)}) copy-start(bf16[4,128,2048]{2,1,0:T(8,128)(2,1)} %param.4) | copy-start | bytes 6291460
  6.5 106.6 %all-gather.2.cloned.1.call-start = ((), (), s32[]{:S(2)}) async-start(), calls=%async_computation.2 | async-start | bytes 17301504 | tf_op jit(solution)/shard_map/all_gather | solution.py:97
  125.1 10.5 %copy-start.1 = (s32[4,4]{1,0:T(4,128)S(1)}, s32[4,4]{1,0:T(4,128)}, u32[]{:S(2)}) copy-start(s32[4,4]{1,0:T(4,128)} %param.6) | copy-start | bytes 196
  129.2 13.1 %all-to-all-start = ((f32[8,3,512]{2,1,0:T(4,128)}), f32[8,3,512]{2,1,0:T(4,128)S(1)}, u32[]{:S(2)}, u32[]{:S(2)}) async-start(f32[8,3,512]{2,1,0:T(4,128)} %broadcast_in_dim.28), calls=%async_computation | async-start | bytes 131072 | tf_op jit(solution)/shard_map/all_to_all | solution.py:13
Sparse Core Ops, SparseCore 0:
  9.2 103.8 all-gather.1
where the time goes:
time: 166 us
  waiting for transfers between devices  112 us (67%)
  blocking collectives  15.7 us (9%)
  between operations  13.5 us (8%)
  matrix products  12 us (7%)
  starting transfers between devices  6.42 us (4%)
  other arithmetic  4.39 us (3%)
  local copies, waits for them, and re-layouts  1.87 us (1%)
    all_gather x1, waiting for transfers between devices, per_device(): block_rows = lax.all_gather(unembedding, 'shadow', axis=0, tiled=True)  105 us
    all_to_all x1, blocking collectives, copy_for_each(): return lax.all_to_all(copies, axis, split_axis=0, concat_axis=0, tiled=True)  15.7 us
    dot_general x1, matrix products, fold_block(): lax.dot_general(flat_rows, block_rows, (((1,), (1,)), ((), ())), preferre...  12 us
    all_to_all x1, waiting for transfers between devices, copy_for_each(): return lax.all_to_all(copies, axis, split_axis=0, concat_axis=0, tiled=True)  6.54 us
    all_to_all x1, starting transfers between devices, copy_for_each(): return lax.all_to_all(copies, axis, split_axis=0, concat_axis=0, tiled=True)  6.42 us
    reduce_sum x1, other arithmetic, fold_block(): summed = jnp.sum(fresh_terms, axis=1)  3.42 us
  transfers between devices with their start and end apart: 2, of which 2 were waited for; matrix products, arithmetic and copies ran while one was open for 0% of the time, Pallas kernels for 0%

commit v1 on v0

--- a/solution.py
+++ b/solution.py
@@ -94,7 +94,9 @@
     slice_start = vocab_index * slice_tokens
     flat_rows = hidden.reshape(shadow_count * token_count, model_width)
     wanted = jnp.tile(targets, shadow_count)
-    block_rows = lax.all_gather(unembedding, "shadow", axis=0, tiled=True)
+    block_rows = jnp.concatenate(
+        lax.all_to_all(jnp.stack([unembedding] * lax.axis_size("shadow")), "shadow", 0, 0), axis=0
+    )
     gathered = jnp.arange(block_rows.shape[0], dtype=jnp.int32)
     vocab_rows = (
         gathered // head_rows * vocab_count + vocab_index

time: 166 us -> 428 us (2.58)
  waiting for transfers between devices: 112 us -> 365 us
  between operations: 13.5 us -> 0.11 us
  starting transfers between devices: 6.42 us -> 17.7 us
  local copies, waits for them, and re-layouts: 1.87 us -> 8.15 us
  blocking collectives: 15.7 us -> 20.7 us
    all_to_all x0 -> x1, waiting for transfers between devices: none -> 359 us  [per_device(): lax.all_to_all(jnp.stack([unembedding] * lax.axis_size('shadow')), 'shado...]
    all_gather x1 -> x0, waiting for transfers between devices: 105 us -> none  [per_device(): block_rows = lax.all_gather(unembedding, 'shadow', axis=0, tiled=True)]
    all_to_all x0 -> x1, starting transfers between devices: none -> 11.3 us  [per_device(): lax.all_to_all(jnp.stack([unembedding] * lax.axis_size('shadow')), 'shado...]
    another operation x0 -> x1, local copies, waits for them, and re-layouts: none -> 6.94 us  [per_device(): jnp.stack([unembedding] * lax.axis_size('shadow'))]
    all_to_all x1, blocking collectives: 15.7 us -> 20.7 us  [copy_for_each(): return lax.all_to_all(copies, axis, split_axis=0, concat_axis=0, tiled=True)]
where the time goes in v1:
time: 428 us
  waiting for transfers between devices  365 us (85%)
  blocking collectives  20.7 us (5%)
  starting transfers between devices  17.7 us (4%)
  matrix products  12 us (3%)
  local copies, waits for them, and re-layouts  8.15 us (2%)
  other arithmetic  4.39 us (1%)
    all_to_all x1, waiting for transfers between devices, per_device(): lax.all_to_all(jnp.stack([unembedding] * lax.axis_size('shadow')), 'shado...  359 us
    all_to_all x1, blocking collectives, copy_for_each(): return lax.all_to_all(copies, axis, split_axis=0, concat_axis=0, tiled=True)  20.7 us
    dot_general x1, matrix products, fold_block(): lax.dot_general(flat_rows, block_rows, (((1,), (1,)), ((), ())), preferre...  12 us
    all_to_all x1, starting transfers between devices, per_device(): lax.all_to_all(jnp.stack([unembedding] * lax.axis_size('shadow')), 'shado...  11.3 us
  transfers between devices with their start and end apart: 2, of which 2 were waited for; matrix products, arithmetic and copies ran while one was open for 0% of the time, Pallas kernels for 0%

profile of v1, /device:TPU:1, one launch (start us, length us, event | category | flops | bytes accessed | tf_op | source)
XLA Modules:
  0.0 428.1 jit_solution(16186461959116896156)
XLA Ops:
  0.0 0.0 copy-start
  0.0 6.9 %stack.2 = bf16[32,128,2048]{2,1,0:T(8,128)(2,1)} broadcast(bf16[128,2048]{1,0:T(8,128)(2,1)} %param.7), dimensions={1,2} | broadcast | bytes 17301504 | tf_op jit(solution)/shard_map/stack | solution.py:98
  6.9 0.0 copy-start.2
  6.9 11.3 %all-to-all-start = ((bf16[32,128,2048]{2,1,0:T(8,128)(2,1)}), bf16[32,128,2048]{2,1,0:T(8,128)(2,1)}, u32[]{:S(2)}, u32[]{:S(2)}) async-start(bf16[32,128,2048]{2,1,0:T(8,128)(2,1)} %stack.2), calls=%async_computation | async-start | bytes 33554432 | tf_op jit(solution)/shard_map/all_to_all | solution.py:98
  18.3 0.0 copy-done.2
  18.3 358.5 %all-to-all-done = bf16[32,128,2048]{2,1,0:T(8,128)(2,1)} async-done(((bf16[32,128,2048]{2,1,0:T(8,128)(2,1)}), bf16[32,128,2048]{2,1,0:T(8,128)(2,1)}, u32[]{:S(2)}, u32[]{:S(2)}) %all-to-all-start) | async-done | bytes 16777248 | tf_op jit(solution)/shard_map/all_to_all | solution.py:98
  376.8 0.0 copy-done
  376.8 12.0 %fusion.2 = (f32[512]{0:T(512)S(1)}, f32[512,4096]{1,0:T(8,128)S(1)}) fusion(s32[4096]{0:T(1024)S(1)} %fusion.12, s32[512]{0:T(512)S(1)} %broadcast_bitcast_fusion, bf16[512,2048]{1,0:T(8,128)(2,1)S(1)} %bitcast.18, bf16[4096,2048]{1,0:T(8,128)(2,1)} %bitcast.2), kind=kOutput, calls=%fused_computation.5 | convolution fusion | flops 8596226048 | bytes 27283456 | tf_op jit(solution)/shard_map/dot_general | solution.py:69
  388.9 0.0 copy-start.1
  388.9 3.4 fusion
  392.3 0.6 broadcast_in_dim.28
  393.0 6.4 %all-to-all-start.1 = ((f32[8,3,512]{2,1,0:T(4,128)}), f32[8,3,512]{2,1,0:T(4,128)S(1)}, u32[]{:S(2)}, u32[]{:S(2)}) async-start(f32[8,3,512]{2,1,0:T(4,128)} %broadcast_in_dim.28), calls=%async_computation.1 | async-start | bytes 131072 | tf_op jit(solution)/shard_map/all_to_all | solution.py:13
  399.3 0.0 copy-done.1
  399.3 0.1 broadcast_in_dim.29
  399.4 0.1 reshape.85
  399.5 6.5 %all-to-all-done.1 = f32[8,3,512]{2,1,0:T(4,128)S(1)} async-done(((f32[8,3,512]{2,1,0:T(4,128)}), f32[8,3,512]{2,1,0:T(4,128)S(1)}, u32[]{:S(2)}, u32[]{:S(2)}) %all-to-all-start.1) | async-done | bytes 49184 | tf_op jit(solution)/shard_map/all_to_all | solution.py:13
  406.5 0.1 fusion.17
  406.6 0.1 pad_maximum_fusion.1
  406.6 20.7 %all_to_all.16 = f32[32,1,32]{2,1,0:T(1,128)S(1)} all-to-all(f32[32,1,32]{2,1,0:T(1,128)S(1)} %broadcast_in_dim.30), channel_id=1, replica_groups=mesh['shadow'=32,'vocab'=8] {'shadow'}, dimensions={0} | all-to-all | bytes 8192 | tf_op jit(solution)/shard_map/all_to_all | solution.py:13
  427.4 0.1 fusion.21
  427.5 0.7 rsqrt_multiply_fusion
  (26 shorter events, 0.5 us)
Async XLA Ops:
  0.0 376.8 %copy-start = (bf16[4,128,2048]{2,1,0:T(8,128)(2,1)S(1)}, bf16[4,128,2048]{2,1,0:T(8,128)(2,1)}, u32[]{:S(2)}) copy-start(bf16[4,128,2048]{2,1,0:T(8,128)(2,1)} %param.4) | copy-start | bytes 6291460
  6.9 11.3 %copy-start.2 = (s32[128]{0:T(128)S(1)}, s32[128]{0:T(128)}, u32[]{:S(2)}) copy-start(s32[128]{0:T(128)} %param.5) | copy-start | bytes 1540
  6.9 369.9 %all-to-all-start = ((bf16[32,128,2048]{2,1,0:T(8,128)(2,1)}), bf16[32,128,2048]{2,1,0:T(8,128)(2,1)}, u32[]{:S(2)}, u32[]{:S(2)}) async-start(bf16[32,128,2048]{2,1,0:T(8,128)(2,1)} %stack.2), calls=%async_computation | async-start | bytes 33554432 | tf_op jit(solution)/shard_map/all_to_all | solution.py:98
  388.9 10.5 %copy-start.1 = (s32[4,4]{1,0:T(4,128)S(1)}, s32[4,4]{1,0:T(4,128)}, u32[]{:S(2)}) copy-start(s32[4,4]{1,0:T(4,128)} %param.6) | copy-start | bytes 196
  393.0 13.1 %all-to-all-start.1 = ((f32[8,3,512]{2,1,0:T(4,128)}), f32[8,3,512]{2,1,0:T(4,128)S(1)}, u32[]{:S(2)}, u32[]{:S(2)}) async-start(f32[8,3,512]{2,1,0:T(4,128)} %broadcast_in_dim.28), calls=%async_computation.1 | async-start | bytes 131072 | tf_op jit(solution)/shard_map/all_to_all | solution.py:13
